TPU v7x, 32 devices: a whole 2x2x4 slice. The times are simulated.
32 devices in a mesh: tm: 8 (over z, y), space: 4 (over x, core).
Axes of the slice: x: 2, y: 2, z: 4, core: 2. Of those that a mesh axis runs over, the one named last changes fastest.
Arguments:
- starts: float32 [8, 5, 16, 64, 128], P('tm', None, 'space'), may hold values from -4 to 4
- source: float32 [5, 16, 64, 128], P(None, 'space'), may hold values from -4 to 4
Outputs:
- ends: float32 [8, 5, 16, 64, 128], P('tm', None, 'space')
- slice_norms: float32 [8], P('tm')
- total_norm: float32 [1], replicated
All inputs are finite; a program needn't handle non-finite values.
Results may differ from a plain program's by a relative error of at most 0.0003.
Values sent between devices are 32-bit elements; how exact they have to be, the bound alone decides.
A program may use at most 64 MiB of HBM per device.

v0:
```python
import math
import jax
import jax.numpy as jnp
from jax import lax
from jax.sharding import PartitionSpec as P

viscosity = 0.08
diffusivity = 0.05
compress_rate = 0.25
time_step = 0.5
diffusion_number = 0.08
advect_xaxis = 0.2
advect_yaxis = 0.15
advect_zaxis = 0.1
epsilon = 1e-06
highest = lax.Precision.HIGHEST


def with_halo(cells, sides, width):
    for axis, dim in sides:
        count = lax.axis_size(axis)
        head = lax.slice_in_dim(cells, 0, width, axis=dim)
        tail = lax.slice_in_dim(cells, cells.shape[dim] - width, cells.shape[dim], axis=dim)
        cells = jnp.concatenate(
            [
                lax.ppermute(tail, axis, [(i, (i + 1) % count) for i in range(count)]),
                cells,
                lax.ppermute(head, axis, [((i + 1) % count, i) for i in range(count)]),
            ],
            axis=dim,
        )
    return cells


def across(values, axis):
    return 0.5 * (jnp.roll(values, -1, axis) - jnp.roll(values, 1, axis))


def vertical(values):
    return 0.5 * (values[2:] - values[:-2])


def laplace(values):
    interior = values[1:-1]
    summed = values[2:] + values[:-2] - 6.0 * interior
    for axis in (1, 2):
        summed = summed + jnp.roll(interior, -1, axis) + jnp.roll(interior, 1, axis)
    return summed


def tendency(padded, source):
    speed_xaxis = advect_xaxis + padded[0]
    speed_yaxis = advect_yaxis + padded[1]
    speed_zaxis = advect_zaxis + padded[2]

    def transport(quantity):
        return (
            across((speed_xaxis * quantity)[1:-1], 2)
            + across((speed_yaxis * quantity)[1:-1], 1)
            + vertical(speed_zaxis * quantity)
        )

    pressure = padded[3]
    xmomentum = -transport(padded[0]) - across(pressure[1:-1], 2) + viscosity * laplace(padded[0])
    ymomentum = -transport(padded[1]) - across(pressure[1:-1], 1) + viscosity * laplace(padded[1])
    zmomentum = -transport(padded[2]) - vertical(pressure) + viscosity * laplace(padded[2])
    pressure_rate = -compress_rate * (
        across(padded[0][1:-1], 2) + across(padded[1][1:-1], 1) + vertical(padded[2])
    )
    scalar_rate = -transport(padded[4]) + diffusivity * laplace(padded[4])
    return jnp.stack([xmomentum, ymomentum, zmomentum, pressure_rate, scalar_rate]) + source


def slab_rates(current, source):
    padded = with_halo(current, (("space", 1),), 1)
    return tendency(padded, source)


def kept_modes(keep):
    mode_ids = jnp.arange(2 * keep, dtype=jnp.int32)
    return jnp.where(mode_ids < keep, mode_ids, mode_ids - 2 * keep)


def wave_table(cell_ids, mode_ids, length):
    products = cell_ids[:, None] * mode_ids[None, :] % length
    angles = 2.0 * math.pi / length * products.astype(jnp.float32)
    return (jnp.cos(angles), jnp.sin(angles))


def shards(starts, source):
    state_now = starts[0]
    fields, slab_depth, grid_rows, grid_cols = state_now.shape
    width_space = lax.axis_size("space")
    width_time = lax.axis_size("tm")
    grid_depth = slab_depth * width_space
    keep_y = grid_rows // 8
    keep_x = grid_cols // 16
    mode_count = 4 * keep_y * keep_x
    current = state_now
    section_one = slab_rates(current, source)
    section_two = slab_rates(current + 0.5 * time_step * section_one, source)
    section_three = slab_rates(current + 0.5 * time_step * section_two, source)
    section_four = slab_rates(current + time_step * section_three, source)
    current = current + time_step / 6.0 * (
        section_one + 2.0 * section_two + 2.0 * section_three + section_four
    )
    xmodes = kept_modes(keep_x)
    ymodes = kept_modes(keep_y)
    xcosines, xsines = wave_table(jnp.arange(grid_cols, dtype=jnp.int32), xmodes, grid_cols)
    ycosines, ysines = wave_table(jnp.arange(grid_rows, dtype=jnp.int32), ymodes, grid_rows)
    stacked = jnp.stack([current, state_now]).reshape(2 * fields, slab_depth, grid_rows, grid_cols)
    real_x = jnp.einsum("bzyx,xk->bzyk", stacked, xcosines, precision=highest)
    imag_x = -jnp.einsum("bzyx,xk->bzyk", stacked, xsines, precision=highest)
    real_y = jnp.einsum("bzyk,yj->bzjk", real_x, ycosines, precision=highest) + jnp.einsum(
        "bzyk,yj->bzjk", imag_x, ysines, precision=highest
    )
    imag_y = jnp.einsum("bzyk,yj->bzjk", imag_x, ycosines, precision=highest) - jnp.einsum(
        "bzyk,yj->bzjk", real_x, ysines, precision=highest
    )
    real_y = real_y.reshape(2 * fields, slab_depth, mode_count)
    imag_y = imag_y.reshape(2 * fields, slab_depth, mode_count)
    space_pos = lax.axis_index("space")
    zcells = space_pos * slab_depth + jnp.arange(slab_depth, dtype=jnp.int32)
    zwaves = jnp.arange(lax.axis_size("space") * slab_depth, dtype=jnp.int32)
    zcosines, zsines = wave_table(zwaves, zcells, grid_depth)
    term_real = jnp.einsum("qz,bzm->qbm", zcosines, real_y, precision=highest) + jnp.einsum(
        "qz,bzm->qbm", zsines, imag_y, precision=highest
    )
    term_imag = jnp.einsum("qz,bzm->qbm", zcosines, imag_y, precision=highest) - jnp.einsum(
        "qz,bzm->qbm", zsines, real_y, precision=highest
    )
    spectrum = lax.psum_scatter(
        jnp.stack([term_real, term_imag], axis=1), "space", scatter_dimension=0, tiled=True
    )
    zangles = 2.0 * math.pi / grid_depth * zcells.astype(jnp.float32)
    yangles = 2.0 * math.pi / grid_rows * ymodes.astype(jnp.float32)
    xangles = 2.0 * math.pi / grid_cols * xmodes.astype(jnp.float32)
    keeper = (
        ((ymodes != -keep_y)[:, None] & (xmodes != -keep_x)[None, :])
        .astype(jnp.float32)
        .reshape(mode_count)
    )
    plane_cos = (
        (2.0 * jnp.cos(yangles) - 2.0)[:, None] + (2.0 * jnp.cos(xangles) - 2.0)[None, :]
    ).reshape(mode_count)
    plane_sin = (
        advect_yaxis * jnp.sin(yangles)[:, None] + advect_xaxis * jnp.sin(xangles)[None, :]
    ).reshape(mode_count)
    sym_real = (
        1.0 + diffusion_number * ((2.0 * jnp.cos(zangles) - 2.0)[:, None] + plane_cos[None, :])
    ) * keeper[None, :]
    sym_imag = -(advect_zaxis * jnp.sin(zangles)[:, None] + plane_sin[None, :]) * keeper[None, :]
    sym_real = sym_real[:, None, :]
    sym_imag = sym_imag[:, None, :]
    log_size = jnp.where(
        keeper[None, None, :] > 0.0,
        0.5 * jnp.log(sym_real * sym_real + sym_imag * sym_imag + (1.0 - keeper[None, None, :])),
        -60.0,
    )
    turning = jnp.arctan2(sym_imag, sym_real)
    fine_real = spectrum[:, 0, :fields]
    fine_imag = spectrum[:, 1, :fields]
    start_real = spectrum[:, 0, fields:]
    start_imag = spectrum[:, 1, fields:]
    position = lax.axis_index("tm")
    later_flag = (position > 0).astype(jnp.float32)
    coarse_real = sym_real * start_real - sym_imag * start_imag
    coarse_imag = sym_real * start_imag + sym_imag * start_real
    jumps = jnp.stack([fine_real - later_flag * coarse_real, fine_imag - later_flag * coarse_imag])
    portion = lax.all_gather(jumps[None], "tm", axis=0, tiled=True)
    source_rows = jnp.arange(portion.shape[0], dtype=jnp.int32)
    gaps = position - 1 - source_rows
    live = (gaps >= 0).astype(jnp.float32)[:, None, None, None]
    exponent = jnp.maximum(gaps, 0).astype(jnp.float32)[:, None, None, None]
    damping = live * jnp.exp(exponent * log_size[None])
    cosine = damping * jnp.cos(exponent * turning[None])
    sine_part = damping * jnp.sin(exponent * turning[None])
    added_real = jnp.sum(cosine * portion[:, 0] - sine_part * portion[:, 1], axis=0)
    added_imag = jnp.sum(cosine * portion[:, 1] + sine_part * portion[:, 0], axis=0)
    prior_sum = jnp.stack([added_real, added_imag])
    diff_real = prior_sum[0] - later_flag * start_real
    diff_imag = prior_sum[1] - later_flag * start_imag
    spectral_fix = jnp.stack(
        [sym_real * diff_real - sym_imag * diff_imag, sym_real * diff_imag + sym_imag * diff_real],
        axis=1,
    )
    portion = lax.all_gather(spectral_fix, "space", axis=0, tiled=True)
    zwaves = jnp.arange(portion.shape[0], dtype=jnp.int32)
    zcosines, zsines = wave_table(zcells, zwaves, grid_depth)
    back_real = jnp.einsum("zq,qfm->zfm", zcosines, portion[:, 0], precision=highest) - jnp.einsum(
        "zq,qfm->zfm", zsines, portion[:, 1], precision=highest
    )
    back_imag = jnp.einsum("zq,qfm->zfm", zcosines, portion[:, 1], precision=highest) + jnp.einsum(
        "zq,qfm->zfm", zsines, portion[:, 0], precision=highest
    )
    local_depth = jnp.stack([back_real, back_imag], axis=1)
    planes = local_depth.reshape(slab_depth, 2, fields, 2 * keep_y, 2 * keep_x)
    plane_real = jnp.einsum(
        "zfjk,yj->zfyk", planes[:, 0], ycosines, precision=highest
    ) - jnp.einsum("zfjk,yj->zfyk", planes[:, 1], ysines, precision=highest)
    plane_imag = jnp.einsum(
        "zfjk,yj->zfyk", planes[:, 1], ycosines, precision=highest
    ) + jnp.einsum("zfjk,yj->zfyk", planes[:, 0], ysines, precision=highest)
    correction = (
        jnp.einsum("zfyk,xk->fzyx", plane_real, xcosines, precision=highest)
        - jnp.einsum("zfyk,xk->fzyx", plane_imag, xsines, precision=highest)
    ) / (grid_depth * grid_rows * grid_cols)
    end_states = current + correction
    local_sum = jnp.sum(correction * correction)
    cell_total = fields * grid_depth * grid_rows * grid_cols
    slice_sum = lax.psum(local_sum, "space")
    every_sum = lax.psum(slice_sum, "tm")
    slice_value = jnp.sqrt(slice_sum / cell_total + epsilon).reshape(1)
    total_value = jnp.sqrt(every_sum / (cell_total * width_time) + epsilon).reshape(1)
    return (end_states[None], slice_value, total_value)


def solution(mesh):
    in_specs = (P("tm", None, "space", None, None), P(None, "space", None, None))
    out_specs = (P("tm", None, "space", None, None), P("tm"), P())
    return jax.shard_map(shards, mesh=mesh, in_specs=in_specs, out_specs=out_specs, check_vma=False)
```

profile of v0, /device:TPU:0, one launch (start us, length us, event | category | flops | bytes accessed | tf_op | source)
XLA Modules:
  0.0 202.2 jit_solution(17779550570251596355)
XLA Ops:
  7.2 1.8 fusion.450
  9.0 0.5 collective-permute-start
  9.5 1.9 collective-permute-start.1
  11.4 1.2 slice_bitcast_fusion.17
  12.6 0.8 slice_bitcast_fusion.51
  13.4 0.8 slice_bitcast_fusion.50
  14.4 0.8 slice_bitcast_fusion.48
  15.2 0.8 fusion.568
  16.0 0.9 fusion.569
  16.9 0.9 fusion.571
  17.8 0.6 sine_multiply_fusion.2
  18.4 0.6 multiply_add_fusion.5
  19.0 0.6 sine_multiply_fusion
  19.8 0.6 broadcast_subtract_fusion
  20.4 0.5 broadcast_compare_fusion
  20.9 0.7 broadcast_add_fusion.1
  21.7 0.8 broadcast_add_fusion
  22.5 0.7 add.1066
  23.2 0.8 multiply_select_fusion
  24.0 1.2 dynamic-slice
  25.9 0.5 maximum_convert_fusion
  28.0 0.5 copy-done.7
  29.2 0.6 copy-done.2
  30.3 0.6 copy-done.13
  31.6 0.8 copy-done.1
  33.7 0.7 collective-permute-start.2
  34.4 1.1 collective-permute-start.3
  35.5 3.0 %collective-permute-done.2 = f32[5,1,64,128]{3,2,1,0:T(8,128)S(1)} collective-permute-done((f32[5,1,64,128]{3,2,1,0:T(8,128)S(1)}, f32[5,1,64,128]{3,2,1,0:T(8,128)S(1)}, u32[]{:S(2)}, u32[]{:S(2)}) %collective-permute-start.2) | collective-permute-done | bytes 163872 | tf_op jit(solution)/shard_map/ppermute | solution.py:26
  38.5 1.6 collective-permute-done.3
  44.1 0.9 collective-permute-start.4
  45.0 1.4 collective-permute-start.5
  46.4 2.9 %collective-permute-done.4 = f32[5,1,64,128]{3,2,1,0:T(8,128)S(1)} collective-permute-done((f32[5,1,64,128]{3,2,1,0:T(8,128)S(1)}, f32[5,1,64,128]{3,2,1,0:T(8,128)S(1)}, u32[]{:S(2)}, u32[]{:S(2)}) %collective-permute-start.4) | collective-permute-done | bytes 163872 | tf_op jit(solution)/shard_map/ppermute | solution.py:26
  49.3 1.3 collective-permute-done.5
  53.5 0.4 multiply_add_fusion
  55.2 0.9 collective-permute-start.6
  56.1 1.3 collective-permute-start.7
  57.4 2.8 %collective-permute-done.6 = f32[5,1,64,128]{3,2,1,0:T(8,128)S(1)} collective-permute-done((f32[5,1,64,128]{3,2,1,0:T(8,128)S(1)}, f32[5,1,64,128]{3,2,1,0:T(8,128)S(1)}, u32[]{:S(2)}, u32[]{:S(2)}) %collective-permute-start.6) | collective-permute-done | bytes 163872 | tf_op jit(solution)/shard_map/ppermute | solution.py:26
  60.2 1.2 collective-permute-done.7
  64.5 3.2 %fusion.304 = f32[10,4,64,16]{2,3,1,0:T(8,128)S(1)} fusion(f32[10,4,64,128]{3,2,1,0:T(8,128)S(1)} %bitcast.754, s32[16]{0:T(128)S(1)} %compare_select_fusion), kind=kOutput, calls=%fused_computation.540 | convolution fusion | flops 62943232 | bytes 1474624 | tf_op jit(solution)/shard_map/bzyx,xk->bzyk/dot_general | solution.py:112
  67.7 3.2 %convolution_negate_fusion = f32[10,4,64,16]{2,3,1,0:T(8,128)S(1)} fusion(f32[10,4,64,128]{3,2,1,0:T(8,128)S(1)} %bitcast.755, s32[16]{0:T(128)S(1)} %compare_select_fusion), kind=kOutput, calls=%fused_computation.8 | convolution fusion | flops 62984192 | bytes 1474624 | tf_op jit(solution)/shard_map/bzyx,xk->bzyk/dot_general | solution.py:113
  70.9 2.5 %fusion.310 = f32[16,10,4,16]{3,0,2,1:T(8,128)S(1)} fusion(f32[10,4,64,16]{2,3,1,0:T(8,128)S(1)} %fusion.304, s32[16]{0:T(128)S(1)} %compare_select_fusion), kind=kOutput, calls=%fused_computation.546 | convolution fusion | flops 7878656 | bytes 204864 | tf_op jit(solution)/shard_map/bzyk,yj->bzjk/dot_general | solution.py:114
  73.4 2.5 %fusion.308 = f32[16,10,4,16]{3,0,2,1:T(8,128)S(1)} fusion(f32[10,4,64,16]{2,3,1,0:T(8,128)S(1)} %convolution_negate_fusion, s32[16]{0:T(128)S(1)} %compare_select_fusion), kind=kOutput, calls=%fused_computation.544 | convolution fusion | flops 7878656 | bytes 204864 | tf_op jit(solution)/shard_map/bzyk,yj->bzjk/dot_general | solution.py:117
  75.9 2.5 %fusion.3 = f32[10,4,16,16]{3,2,1,0:T(8,128)S(1)} fusion(f32[16,10,4,16]{3,0,2,1:T(8,128)S(1)} %fusion.310, f32[10,4,64,16]{2,3,1,0:T(8,128)S(1)} %convolution_negate_fusion, s32[16]{0:T(128)S(1)} %compare_select_fusion), kind=kOutput, calls=%fused_computation.7 | convolution fusion | flops 7888896 | bytes 245824 | tf_op jit(solution)/shard_map/bzyk,yj->bzjk/dot_general | solution.py:114
  78.6 2.5 %fusion.2 = f32[10,4,16,16]{3,2,1,0:T(8,128)S(1)} fusion(f32[16,10,4,16]{3,0,2,1:T(8,128)S(1)} %fusion.308, f32[10,4,64,16]{2,3,1,0:T(8,128)S(1)} %fusion.304, s32[16]{0:T(128)S(1)} %compare_select_fusion), kind=kOutput, calls=%fused_computation.5 | convolution fusion | flops 7888896 | bytes 245824 | tf_op jit(solution)/shard_map/bzyk,yj->bzjk/dot_general | solution.py:117
  81.3 0.5 fusion.346
  81.8 0.5 fusion.344
  82.3 0.5 fusion.7
  82.8 0.5 fusion.6
  83.3 0.7 pad_maximum_fusion.1
  84.1 0.3 fusion.282
  84.4 32.7 %all-reduce.3.cloned.1.call-done = f32[16,2,10,256]{3,0,2,1:T(8,128)} async-done(((f32[16,2,10,256]{3,0,2,1:T(8,128)}), f32[16,2,10,256]{3,0,2,1:T(8,128)}) %all-reduce.3.cloned.1.call-update) | async-done | bytes 327696
  117.1 0.9 fusion.285
  118.0 31.1 %all-gather = f32[16,4,5,256]{3,1,2,0:T(4,128)S(1)} all-gather(f32[2,4,5,256]{3,1,2,0:T(4,128)S(1)} %pad_maximum_fusion.26), channel_id=2, replica_groups=mesh['tm'=8,'space'=4] {'tm'}, dimensions={0}, use_global_device_ids=true | all-gather | bytes 368640 | tf_op jit(solution)/shard_map/all_gather | solution.py:170
  149.2 0.8 multiply_subtract_fusion
  150.1 5.7 %all_gather.7 = f32[16,2,5,256]{3,1,2,0:T(2,128)S(1)} all-gather(f32[4,2,5,256]{3,1,2,0:T(2,128)S(1)} %copy.243), channel_id=1, replica_groups=mesh['tm'=8,'space'=4] {'space'}, dimensions={0}, use_global_device_ids=true | all-gather | bytes 204800 | tf_op jit(solution)/shard_map/all_gather | solution.py:187
  157.0 0.5 fusion.13
  157.9 0.5 fusion.17
  158.4 0.5 fusion.4
  158.8 0.5 fusion.5
  159.3 1.2 fusion.302
  160.5 1.8 multiply_reduce_fusion
  162.4 6.6 %psum.14 = f32[]{:T(128)} all-reduce(f32[]{:T(128)} %get-tuple-element.60), channel_id=1, replica_groups=mesh['tm'=8,'space'=4] {'space'}, use_global_device_ids=true, to_apply=%region_4.5 | all-reduce | flops 1 | bytes 8 | tf_op jit(solution)/shard_map/psum | solution.py:211
  169.0 0.9 copy.250
  169.9 21.8 %psum.15 = f32[]{:T(128)} all-reduce(f32[]{:T(128)} %psum.14), channel_id=1, replica_groups=mesh['tm'=8,'space'=4] {'tm'}, use_global_device_ids=true, to_apply=%region_5.6 | all-reduce | flops 1 | bytes 8 | tf_op jit(solution)/shard_map/psum | solution.py:212
  (229 shorter events, 17.3 us)
Async XLA Ops:
  7.2 110.0 %all-reduce.3.cloned.1.call-start = ((), (), s32[]{:S(2)}) async-start(), calls=%async_computation | async-start | bytes 655360
  9.0 17.5 %collective-permute-start = (f32[5,1,64,128]{3,2,1,0:T(8,128)}, f32[5,1,64,128]{3,2,1,0:T(8,128)S(1)}, u32[]{:S(2)}, u32[]{:S(2)}) collective-permute-start(f32[5,1,64,128]{3,2,1,0:T(8,128)} %get-tuple-element.91), channel_id=1, source_target_pairs={{0,1},{1,2},{2,3},{3,0},{4,5},{5,6},{6,7},{7,4},{8,9},{9,10},{10,1... | collective-permute-start | bytes 491528 | tf_op jit(solution)/shard_map/ppermute | solution.py:26
  9.5 17.0 %collective-permute-start.1 = (f32[5,1,64,128]{3,2,1,0:T(8,128)}, f32[5,1,64,128]{3,2,1,0:T(8,128)S(1)}, u32[]{:S(2)}, u32[]{:S(2)}) collective-permute-start(f32[5,1,64,128]{3,2,1,0:T(8,128)} %get-tuple-element.90), channel_id=1, source_target_pairs={{1,0},{2,1},{3,2},{0,3},{5,4},{6,5},{7,6},{4,7},{9,8},{10,9},{11,1... | collective-permute-start | bytes 491528 | tf_op jit(solution)/shard_map/ppermute | solution.py:28
  16.0 10.4 %copy-start = (f32[1,5,4,64,128]{4,3,2,1,0:T(8,128)S(1)}, f32[1,5,4,64,128]{4,3,2,1,0:T(8,128)}, u32[]{:S(2)}) copy-start(f32[1,5,4,64,128]{4,3,2,1,0:T(8,128)} %param.2) | copy-start | bytes 1966084
  27.6 0.9 copy-start.7
  27.6 1.0 copy-start.8
  27.6 1.0 copy-start.9
  27.7 1.1 copy-start.10
  27.7 1.1 copy-start.11
  27.7 1.2 copy-start.12
  28.8 0.9 copy-start.2
  28.8 1.0 copy-start.3
  28.8 1.0 copy-start.4
  28.8 1.1 copy-start.5
  28.9 1.2 copy-start.6
  30.0 0.9 copy-start.13
  30.0 1.0 copy-start.14
  30.0 1.0 copy-start.15
  30.0 1.1 copy-start.16
  30.0 1.2 copy-start.17
  30.0 1.2 copy-start.18
  31.4 1.1 copy-start.1
  33.7 4.8 %collective-permute-start.2 = (f32[5,1,64,128]{3,2,1,0:T(8,128)S(1)}, f32[5,1,64,128]{3,2,1,0:T(8,128)S(1)}, u32[]{:S(2)}, u32[]{:S(2)}) collective-permute-start(f32[5,1,64,128]{3,2,1,0:T(8,128)S(1)} %get-tuple-element.84), channel_id=1, source_target_pairs={{0,1},{1,2},{2,3},{3,0},{4,5},{5,6},{6,7},{7,4},{8,9},{9,10},{10,1... | collective-permute-start | bytes 491528 | tf_op jit(solution)/shard_map/ppermute | solution.py:26
  34.4 5.7 %collective-permute-start.3 = (f32[5,1,64,128]{3,2,1,0:T(8,128)S(1)}, f32[5,1,64,128]{3,2,1,0:T(8,128)S(1)}, u32[]{:S(2)}, u32[]{:S(2)}) collective-permute-start(f32[5,1,64,128]{3,2,1,0:T(8,128)S(1)} %get-tuple-element.83), channel_id=1, source_target_pairs={{1,0},{2,1},{3,2},{0,3},{5,4},{6,5},{7,6},{4,7},{9,8},{10,9},{11,1... | collective-permute-start | bytes 491528 | tf_op jit(solution)/shard_map/ppermute | solution.py:28
  44.1 5.2 %collective-permute-start.4 = (f32[5,1,64,128]{3,2,1,0:T(8,128)S(1)}, f32[5,1,64,128]{3,2,1,0:T(8,128)S(1)}, u32[]{:S(2)}, u32[]{:S(2)}) collective-permute-start(f32[5,1,64,128]{3,2,1,0:T(8,128)S(1)} %get-tuple-element.76), channel_id=1, source_target_pairs={{0,1},{1,2},{2,3},{3,0},{4,5},{5,6},{6,7},{7,4},{8,9},{9,10},{10,1... | collective-permute-start | bytes 491528 | tf_op jit(solution)/shard_map/ppermute | solution.py:26
  45.0 5.6 %collective-permute-start.5 = (f32[5,1,64,128]{3,2,1,0:T(8,128)S(1)}, f32[5,1,64,128]{3,2,1,0:T(8,128)S(1)}, u32[]{:S(2)}, u32[]{:S(2)}) collective-permute-start(f32[5,1,64,128]{3,2,1,0:T(8,128)S(1)} %get-tuple-element.75), channel_id=1, source_target_pairs={{1,0},{2,1},{3,2},{0,3},{5,4},{6,5},{7,6},{4,7},{9,8},{10,9},{11,1... | collective-permute-start | bytes 491528 | tf_op jit(solution)/shard_map/ppermute | solution.py:28
  55.2 5.0 %collective-permute-start.6 = (f32[5,1,64,128]{3,2,1,0:T(8,128)S(1)}, f32[5,1,64,128]{3,2,1,0:T(8,128)S(1)}, u32[]{:S(2)}, u32[]{:S(2)}) collective-permute-start(f32[5,1,64,128]{3,2,1,0:T(8,128)S(1)} %get-tuple-element.68), channel_id=1, source_target_pairs={{0,1},{1,2},{2,3},{3,0},{4,5},{5,6},{6,7},{7,4},{8,9},{9,10},{10,1... | collective-permute-start | bytes 491528 | tf_op jit(solution)/shard_map/ppermute | solution.py:26
  56.1 5.3 %collective-permute-start.7 = (f32[5,1,64,128]{3,2,1,0:T(8,128)S(1)}, f32[5,1,64,128]{3,2,1,0:T(8,128)S(1)}, u32[]{:S(2)}, u32[]{:S(2)}) collective-permute-start(f32[5,1,64,128]{3,2,1,0:T(8,128)S(1)} %get-tuple-element.67), channel_id=1, source_target_pairs={{1,0},{2,1},{3,2},{0,3},{5,4},{6,5},{7,6},{4,7},{9,8},{10,9},{11,1... | collective-permute-start | bytes 491528 | tf_op jit(solution)/shard_map/ppermute | solution.py:28
  81.1 3.0 %copy-start.19 = (f32[8]{0:T(128)S(1)}, f32[8]{0:T(128)}, u32[]{:S(2)}) copy-start(f32[8]{0:T(128)} %maximum_convert_fusion) | copy-start | bytes 100
Sparse Core Ops, SparseCore 0:
  84.2 32.9 all-reduce.2
where the time goes:
time: 203 us; the launch traced here: 202 us
  blocking collectives  65.3 us (32%)
  waiting for transfers between devices  45.6 us (22%)
  matrix products  24.5 us (12%)
  local copies, waits for them, and re-layouts  22.2 us (11%)
  between operations  19.9 us (10%)
  other arithmetic  16 us (8%)
  starting transfers between devices  8.72 us (4%)
    unnamed x2, waiting for transfers between devices  32.7 us
    all_gather x1, blocking collectives, shards(): portion = lax.all_gather(jumps[None], 'tm', axis=0, tiled=True)  31.1 us
    psum x1, blocking collectives, shards(): every_sum = lax.psum(slice_sum, 'tm')  21.8 us
    ppermute x4, waiting for transfers between devices, with_halo(): lax.ppermute(tail, axis, [(i, (i + 1) % count) for i in range(count)])  8.68 us
    psum x1, blocking collectives, shards(): slice_sum = lax.psum(local_sum, 'space')  6.61 us
    all_gather x1, blocking collectives, shards(): portion = lax.all_gather(spectral_fix, 'space', axis=0, tiled=True)  5.73 us
    ppermute x4, starting transfers between devices, with_halo(): lax.ppermute(head, axis, [((i + 1) % count, i) for i in range(count)])  5.7 us
    unnamed x42, local copies, waits for them, and re-layouts  5.61 us
  transfers between devices with their start and end apart: 9, of which 7 were waited for; matrix products, arithmetic and copies ran while one was open for 7% of the time, Pallas kernels for 0%

commit v1 on v0

--- a/solution.py
+++ b/solution.py
@@ -14,6 +14,15 @@
 advect_zaxis = 0.1
 epsilon = 1e-06
 highest = lax.Precision.HIGHEST
+
+
+def doubling_sum(block, axis):
+    size = lax.axis_size(axis)
+    total, far = (block, 1)
+    while far < size:
+        total = total + lax.ppermute(total, axis, [(i, i ^ far) for i in range(size)])
+        far = 2 * far
+    return total
 
 
 def with_halo(cells, sides, width):
@@ -209,7 +218,7 @@
     local_sum = jnp.sum(correction * correction)
     cell_total = fields * grid_depth * grid_rows * grid_cols
     slice_sum = lax.psum(local_sum, "space")
-    every_sum = lax.psum(slice_sum, "tm")
+    every_sum = doubling_sum(slice_sum, "tm")
     slice_value = jnp.sqrt(slice_sum / cell_total + epsilon).reshape(1)
     total_value = jnp.sqrt(every_sum / (cell_total * width_time) + epsilon).reshape(1)
     return (end_states[None], slice_value, total_value)

time: 203 us -> 193 us (0.951)
  blocking collectives: 65.3 us -> 43.4 us
  starting transfers between devices: 8.72 us -> 14.1 us
  waiting for transfers between devices: 45.6 us -> 50.8 us
    psum x1 -> x0, blocking collectives: 21.8 us -> none  [shards(): every_sum = lax.psum(slice_sum, 'tm')]
    ppermute x0 -> x3, starting transfers between devices: none -> 5.35 us  [doubling_sum(): lax.ppermute(total, axis, [(i, i ^ far) for i in range(size)])]
    ppermute x0 -> x3, waiting for transfers between devices: none -> 5.25 us  [doubling_sum(): lax.ppermute(total, axis, [(i, i ^ far) for i in range(size)])]
  transfers between devices with their start and end apart: 9 -> 12, of which waited for: 7 -> 10; matrix products, arithmetic and copies ran while one was open for 7% -> 8% of each run, Pallas kernels for 0% -> 0%
where the time goes in v1:
time: 193 us; the launch traced here: 192 us
  waiting for transfers between devices  50.8 us (26%)
  blocking collectives  43.4 us (22%)
  matrix products  24.5 us (13%)
  local copies, waits for them, and re-layouts  22.2 us (12%)
  between operations  21.6 us (11%)
  other arithmetic  15.8 us (8%)
  starting transfers between devices  14.1 us (7%)
    unnamed x2, waiting for transfers between devices  32.8 us
    all_gather x1, blocking collectives, shards(): portion = lax.all_gather(jumps[None], 'tm', axis=0, tiled=True)  31.1 us
    ppermute x4, waiting for transfers between devices, with_halo(): lax.ppermute(tail, axis, [(i, (i + 1) % count) for i in range(count)])  8.68 us
    psum x1, blocking collectives, shards(): slice_sum = lax.psum(local_sum, 'space')  6.61 us
    all_gather x1, blocking collectives, shards(): portion = lax.all_gather(spectral_fix, 'space', axis=0, tiled=True)  5.73 us
    ppermute x4, starting transfers between devices, with_halo(): lax.ppermute(head, axis, [((i + 1) % count, i) for i in range(count)])  5.7 us
    unnamed x42, local copies, waits for them, and re-layouts  5.61 us
    ppermute x3, starting transfers between devices, doubling_sum(): lax.ppermute(total, axis, [(i, i ^ far) for i in range(size)])  5.35 us
  transfers between devices with their start and end apart: 12, of which 10 were waited for; matrix products, arithmetic and copies ran while one was open for 8% of the time, Pallas kernels for 0%

profile of v1, /device:TPU:0, one launch (start us, length us, event | category | flops | bytes accessed | tf_op | source)
XLA Modules:
  0.0 192.4 jit_solution(10039134884684870298)
XLA Ops:
  7.2 1.7 fusion.450
  9.0 0.5 collective-permute-start
  9.5 1.9 collective-permute-start.1
  11.4 1.2 slice_bitcast_fusion.17
  12.6 0.8 slice_bitcast_fusion.51
  13.4 0.8 slice_bitcast_fusion.50
  14.4 0.7 slice_bitcast_fusion.48
  15.2 0.9 fusion.568
  16.0 0.9 fusion.569
  16.9 0.8 fusion.571
  17.8 0.6 sine_multiply_fusion.2
  18.4 0.6 multiply_add_fusion.5
  18.9 0.6 sine_multiply_fusion
  19.7 0.6 broadcast_subtract_fusion
  20.3 0.5 broadcast_compare_fusion
  20.8 0.7 broadcast_add_fusion.1
  21.6 0.7 broadcast_add_fusion
  22.3 0.7 add.1073
  22.9 0.8 multiply_select_fusion
  23.8 1.2 dynamic-slice
  25.7 0.5 maximum_convert_fusion
  27.7 0.5 copy-done.7
  28.9 0.6 copy-done.2
  30.1 0.6 copy-done.13
  31.4 0.8 copy-done.1
  33.5 0.7 collective-permute-start.2
  34.2 1.1 collective-permute-start.3
  35.3 3.0 %collective-permute-done.2 = f32[5,1,64,128]{3,2,1,0:T(8,128)S(1)} collective-permute-done((f32[5,1,64,128]{3,2,1,0:T(8,128)S(1)}, f32[5,1,64,128]{3,2,1,0:T(8,128)S(1)}, u32[]{:S(2)}, u32[]{:S(2)}) %collective-permute-start.2) | collective-permute-done | bytes 163872 | tf_op jit(solution)/shard_map/ppermute | solution.py:35
  38.3 1.6 collective-permute-done.3
  43.9 0.9 collective-permute-start.4
  44.8 1.4 collective-permute-start.5
  46.2 2.9 %collective-permute-done.4 = f32[5,1,64,128]{3,2,1,0:T(8,128)S(1)} collective-permute-done((f32[5,1,64,128]{3,2,1,0:T(8,128)S(1)}, f32[5,1,64,128]{3,2,1,0:T(8,128)S(1)}, u32[]{:S(2)}, u32[]{:S(2)}) %collective-permute-start.4) | collective-permute-done | bytes 163872 | tf_op jit(solution)/shard_map/ppermute | solution.py:35
  49.1 1.3 collective-permute-done.5
  55.0 0.9 collective-permute-start.6
  55.9 1.3 collective-permute-start.7
  57.2 2.8 %collective-permute-done.6 = f32[5,1,64,128]{3,2,1,0:T(8,128)S(1)} collective-permute-done((f32[5,1,64,128]{3,2,1,0:T(8,128)S(1)}, f32[5,1,64,128]{3,2,1,0:T(8,128)S(1)}, u32[]{:S(2)}, u32[]{:S(2)}) %collective-permute-start.6) | collective-permute-done | bytes 163872 | tf_op jit(solution)/shard_map/ppermute | solution.py:35
  59.9 1.2 collective-permute-done.7
  64.3 3.2 %fusion.304 = f32[10,4,64,16]{2,3,1,0:T(8,128)S(1)} fusion(f32[10,4,64,128]{3,2,1,0:T(8,128)S(1)} %bitcast.754, s32[16]{0:T(128)S(1)} %compare_select_fusion), kind=kOutput, calls=%fused_computation.540 | convolution fusion | flops 62943232 | bytes 1474624 | tf_op jit(solution)/shard_map/bzyx,xk->bzyk/dot_general | solution.py:121
  67.5 3.2 %convolution_negate_fusion = f32[10,4,64,16]{2,3,1,0:T(8,128)S(1)} fusion(f32[10,4,64,128]{3,2,1,0:T(8,128)S(1)} %bitcast.755, s32[16]{0:T(128)S(1)} %compare_select_fusion), kind=kOutput, calls=%fused_computation.8 | convolution fusion | flops 62984192 | bytes 1474624 | tf_op jit(solution)/shard_map/bzyx,xk->bzyk/dot_general | solution.py:122
  70.7 2.5 %fusion.310 = f32[16,10,4,16]{3,0,2,1:T(8,128)S(1)} fusion(f32[10,4,64,16]{2,3,1,0:T(8,128)S(1)} %fusion.304, s32[16]{0:T(128)S(1)} %compare_select_fusion), kind=kOutput, calls=%fused_computation.546 | convolution fusion | flops 7878656 | bytes 204864 | tf_op jit(solution)/shard_map/bzyk,yj->bzjk/dot_general | solution.py:123
  73.2 2.5 %fusion.308 = f32[16,10,4,16]{3,0,2,1:T(8,128)S(1)} fusion(f32[10,4,64,16]{2,3,1,0:T(8,128)S(1)} %convolution_negate_fusion, s32[16]{0:T(128)S(1)} %compare_select_fusion), kind=kOutput, calls=%fused_computation.544 | convolution fusion | flops 7878656 | bytes 204864 | tf_op jit(solution)/shard_map/bzyk,yj->bzjk/dot_general | solution.py:126
  75.7 2.5 %fusion.3 = f32[10,4,16,16]{3,2,1,0:T(8,128)S(1)} fusion(f32[16,10,4,16]{3,0,2,1:T(8,128)S(1)} %fusion.310, f32[10,4,64,16]{2,3,1,0:T(8,128)S(1)} %convolution_negate_fusion, s32[16]{0:T(128)S(1)} %compare_select_fusion), kind=kOutput, calls=%fused_computation.7 | convolution fusion | flops 7888896 | bytes 245824 | tf_op jit(solution)/shard_map/bzyk,yj->bzjk/dot_general | solution.py:123
  78.3 2.5 %fusion.2 = f32[10,4,16,16]{3,2,1,0:T(8,128)S(1)} fusion(f32[16,10,4,16]{3,0,2,1:T(8,128)S(1)} %fusion.308, f32[10,4,64,16]{2,3,1,0:T(8,128)S(1)} %fusion.304, s32[16]{0:T(128)S(1)} %compare_select_fusion), kind=kOutput, calls=%fused_computation.5 | convolution fusion | flops 7888896 | bytes 245824 | tf_op jit(solution)/shard_map/bzyk,yj->bzjk/dot_general | solution.py:126
  81.0 0.5 fusion.346
  81.5 0.5 fusion.344
  82.0 0.5 fusion.7
  82.6 0.5 fusion.6
  83.1 0.7 pad_maximum_fusion.1
  84.2 32.7 %all-reduce.3.cloned.1.call-done = f32[16,2,10,256]{3,0,2,1:T(8,128)} async-done(((f32[16,2,10,256]{3,0,2,1:T(8,128)}), f32[16,2,10,256]{3,0,2,1:T(8,128)}) %all-reduce.3.cloned.1.call-update) | async-done | bytes 327696
  116.9 0.9 fusion.285
  117.8 31.1 %all-gather = f32[16,4,5,256]{3,1,2,0:T(4,128)S(1)} all-gather(f32[2,4,5,256]{3,1,2,0:T(4,128)S(1)} %pad_maximum_fusion.26), channel_id=2, replica_groups=mesh['tm'=8,'space'=4] {'tm'}, dimensions={0}, use_global_device_ids=true | all-gather | bytes 368640 | tf_op jit(solution)/shard_map/all_gather | solution.py:179
  149.0 0.8 multiply_subtract_fusion
  149.9 5.7 %all_gather.7 = f32[16,2,5,256]{3,1,2,0:T(2,128)S(1)} all-gather(f32[4,2,5,256]{3,1,2,0:T(2,128)S(1)} %copy.243), channel_id=1, replica_groups=mesh['tm'=8,'space'=4] {'space'}, dimensions={0}, use_global_device_ids=true | all-gather | bytes 204800 | tf_op jit(solution)/shard_map/all_gather | solution.py:196
  157.6 0.5 fusion.17
  159.1 1.2 fusion.302
  160.3 1.8 multiply_reduce_fusion
  162.2 6.6 %psum.7 = f32[]{:T(128)} all-reduce(f32[]{:T(128)} %get-tuple-element.60), channel_id=1, replica_groups=mesh['tm'=8,'space'=4] {'space'}, use_global_device_ids=true, to_apply=%region_4.5 | all-reduce | flops 1 | bytes 8 | tf_op jit(solution)/shard_map/psum | solution.py:220
  168.8 1.4 collective-permute-start.8
  170.2 0.9 copy.250
  171.8 0.8 collective-permute-done.8
  173.8 1.4 collective-permute-start.9
  175.1 2.4 %collective-permute-done.9 = f32[]{:T(128)} collective-permute-done((f32[]{:T(128)}, f32[]{:T(128)}, u32[]{:S(2)}, u32[]{:S(2)}) %collective-permute-start.9) | collective-permute-done | bytes 36 | tf_op jit(solution)/shard_map/ppermute | solution.py:23
  178.1 2.6 %collective-permute-start.10 = (f32[]{:T(128)}, f32[]{:T(128)}, u32[]{:S(2)}, u32[]{:S(2)}) collective-permute-start(f32[]{:T(128)} %add.1092), channel_id=1, source_target_pairs={{0,16},{4,20},{8,24},{12,28},{16,0},{20,4},{24,8},{28,12},{1,17},{... | collective-permute-start | bytes 20 | tf_op jit(solution)/shard_map/ppermute | solution.py:23
  180.6 2.1 %collective-permute-done.10 = f32[]{:T(128)} collective-permute-done((f32[]{:T(128)}, f32[]{:T(128)}, u32[]{:S(2)}, u32[]{:S(2)}) %collective-permute-start.10) | collective-permute-done | bytes 36 | tf_op jit(solution)/shard_map/ppermute | solution.py:23
  (234 shorter events, 19.3 us)
Async XLA Ops:
  7.2 109.7 %all-reduce.3.cloned.1.call-start = ((), (), s32[]{:S(2)}) async-start(), calls=%async_computation | async-start | bytes 655360
  9.0 17.2 %collective-permute-start = (f32[5,1,64,128]{3,2,1,0:T(8,128)}, f32[5,1,64,128]{3,2,1,0:T(8,128)S(1)}, u32[]{:S(2)}, u32[]{:S(2)}) collective-permute-start(f32[5,1,64,128]{3,2,1,0:T(8,128)} %get-tuple-element.91), channel_id=1, source_target_pairs={{0,1},{1,2},{2,3},{3,0},{4,5},{5,6},{6,7},{7,4},{8,9},{9,10},{10,1... | collective-permute-start | bytes 491528 | tf_op jit(solution)/shard_map/ppermute | solution.py:35
  9.5 16.7 %collective-permute-start.1 = (f32[5,1,64,128]{3,2,1,0:T(8,128)}, f32[5,1,64,128]{3,2,1,0:T(8,128)S(1)}, u32[]{:S(2)}, u32[]{:S(2)}) collective-permute-start(f32[5,1,64,128]{3,2,1,0:T(8,128)} %get-tuple-element.90), channel_id=1, source_target_pairs={{1,0},{2,1},{3,2},{0,3},{5,4},{6,5},{7,6},{4,7},{9,8},{10,9},{11,1... | collective-permute-start | bytes 491528 | tf_op jit(solution)/shard_map/ppermute | solution.py:37
  16.0 10.2 %copy-start = (f32[1,5,4,64,128]{4,3,2,1,0:T(8,128)S(1)}, f32[1,5,4,64,128]{4,3,2,1,0:T(8,128)}, u32[]{:S(2)}) copy-start(f32[1,5,4,64,128]{4,3,2,1,0:T(8,128)} %param.2) | copy-start | bytes 1966084
  27.4 0.9 copy-start.7
  27.4 1.0 copy-start.8
  27.4 1.0 copy-start.9
  27.4 1.1 copy-start.10
  27.4 1.1 copy-start.11
  27.4 1.2 copy-start.12
  28.6 0.9 copy-start.2
  28.6 1.0 copy-start.3
  28.6 1.0 copy-start.4
  28.6 1.1 copy-start.5
  28.6 1.2 copy-start.6
  29.8 0.9 copy-start.13
  29.8 1.0 copy-start.14
  29.8 1.0 copy-start.15
  29.8 1.1 copy-start.16
  29.8 1.2 copy-start.17
  29.8 1.2 copy-start.18
  31.1 1.1 copy-start.1
  33.5 4.8 %collective-permute-start.2 = (f32[5,1,64,128]{3,2,1,0:T(8,128)S(1)}, f32[5,1,64,128]{3,2,1,0:T(8,128)S(1)}, u32[]{:S(2)}, u32[]{:S(2)}) collective-permute-start(f32[5,1,64,128]{3,2,1,0:T(8,128)S(1)} %get-tuple-element.84), channel_id=1, source_target_pairs={{0,1},{1,2},{2,3},{3,0},{4,5},{5,6},{6,7},{7,4},{8,9},{9,10},{10,1... | collective-permute-start | bytes 491528 | tf_op jit(solution)/shard_map/ppermute | solution.py:35
  34.2 5.7 %collective-permute-start.3 = (f32[5,1,64,128]{3,2,1,0:T(8,128)S(1)}, f32[5,1,64,128]{3,2,1,0:T(8,128)S(1)}, u32[]{:S(2)}, u32[]{:S(2)}) collective-permute-start(f32[5,1,64,128]{3,2,1,0:T(8,128)S(1)} %get-tuple-element.83), channel_id=1, source_target_pairs={{1,0},{2,1},{3,2},{0,3},{5,4},{6,5},{7,6},{4,7},{9,8},{10,9},{11,1... | collective-permute-start | bytes 491528 | tf_op jit(solution)/shard_map/ppermute | solution.py:37
  43.9 5.2 %collective-permute-start.4 = (f32[5,1,64,128]{3,2,1,0:T(8,128)S(1)}, f32[5,1,64,128]{3,2,1,0:T(8,128)S(1)}, u32[]{:S(2)}, u32[]{:S(2)}) collective-permute-start(f32[5,1,64,128]{3,2,1,0:T(8,128)S(1)} %get-tuple-element.76), channel_id=1, source_target_pairs={{0,1},{1,2},{2,3},{3,0},{4,5},{5,6},{6,7},{7,4},{8,9},{9,10},{10,1... | collective-permute-start | bytes 491528 | tf_op jit(solution)/shard_map/ppermute | solution.py:35
  44.8 5.6 %collective-permute-start.5 = (f32[5,1,64,128]{3,2,1,0:T(8,128)S(1)}, f32[5,1,64,128]{3,2,1,0:T(8,128)S(1)}, u32[]{:S(2)}, u32[]{:S(2)}) collective-permute-start(f32[5,1,64,128]{3,2,1,0:T(8,128)S(1)} %get-tuple-element.75), channel_id=1, source_target_pairs={{1,0},{2,1},{3,2},{0,3},{5,4},{6,5},{7,6},{4,7},{9,8},{10,9},{11,1... | collective-permute-start | bytes 491528 | tf_op jit(solution)/shard_map/ppermute | solution.py:37
  55.0 5.0 %collective-permute-start.6 = (f32[5,1,64,128]{3,2,1,0:T(8,128)S(1)}, f32[5,1,64,128]{3,2,1,0:T(8,128)S(1)}, u32[]{:S(2)}, u32[]{:S(2)}) collective-permute-start(f32[5,1,64,128]{3,2,1,0:T(8,128)S(1)} %get-tuple-element.68), channel_id=1, source_target_pairs={{0,1},{1,2},{2,3},{3,0},{4,5},{5,6},{6,7},{7,4},{8,9},{9,10},{10,1... | collective-permute-start | bytes 491528 | tf_op jit(solution)/shard_map/ppermute | solution.py:35
  55.9 5.3 %collective-permute-start.7 = (f32[5,1,64,128]{3,2,1,0:T(8,128)S(1)}, f32[5,1,64,128]{3,2,1,0:T(8,128)S(1)}, u32[]{:S(2)}, u32[]{:S(2)}) collective-permute-start(f32[5,1,64,128]{3,2,1,0:T(8,128)S(1)} %get-tuple-element.67), channel_id=1, source_target_pairs={{1,0},{2,1},{3,2},{0,3},{5,4},{6,5},{7,6},{4,7},{9,8},{10,9},{11,1... | collective-permute-start | bytes 491528 | tf_op jit(solution)/shard_map/ppermute | solution.py:37
  80.8 3.0 %copy-start.19 = (f32[8]{0:T(128)S(1)}, f32[8]{0:T(128)}, u32[]{:S(2)}) copy-start(f32[8]{0:T(128)} %maximum_convert_fusion) | copy-start | bytes 100
  168.8 3.8 %collective-permute-start.8 = (f32[]{:T(128)}, f32[]{:T(128)}, u32[]{:S(2)}, u32[]{:S(2)}) collective-permute-start(f32[]{:T(128)} %psum.7), channel_id=1, source_target_pairs={{0,4},{4,0},{8,12},{12,8},{16,20},{20,16},{24,28},{28,24},{1,5},{5... | collective-permute-start | bytes 20 | tf_op jit(solution)/shard_map/ppermute | solution.py:23
  173.8 3.7 %collective-permute-start.9 = (f32[]{:T(128)}, f32[]{:T(128)}, u32[]{:S(2)}, u32[]{:S(2)}) collective-permute-start(f32[]{:T(128)} %add.1091), channel_id=1, source_target_pairs={{0,8},{4,12},{8,0},{12,4},{16,24},{20,28},{24,16},{28,20},{1,9},{5... | collective-permute-start | bytes 20 | tf_op jit(solution)/shard_map/ppermute | solution.py:23
  178.1 4.6 %collective-permute-start.10 = (f32[]{:T(128)}, f32[]{:T(128)}, u32[]{:S(2)}, u32[]{:S(2)}) collective-permute-start(f32[]{:T(128)} %add.1092), channel_id=1, source_target_pairs={{0,16},{4,20},{8,24},{12,28},{16,0},{20,4},{24,8},{28,12},{1,17},{... | collective-permute-start | bytes 20 | tf_op jit(solution)/shard_map/ppermute | solution.py:23
Sparse Core Ops, SparseCore 0:
  84.0 32.9 all-reduce.2
